TPU v7x, 32 devices: a 4x4x1 block of a 4x4x8 slice. The times are simulated.
32 devices in a mesh: dp: 1 (over z), tp: 4 (over y), pp: 8 (over x, core).
Axes of the slice: x: 4, y: 4, z: 1, core: 2. Of those that a mesh axis runs over, the one named last changes fastest.
The devices are a block of a 4x4x8 slice.
Arguments:
- stage_buf: bfloat16 [8, 16, 512, 1024], P('pp', 'dp', 'tp')
- new_mb: bfloat16 [16, 512, 1024], P('dp', 'tp')
- positions: int32 [512], replicated
- ln_attn: float32 [8, 2, 1024], P('pp')
- ln_mlp: float32 [8, 2, 1024], P('pp')
- w_qkv: bfloat16 [8, 16, 3, 64, 1024], P('pp', 'tp')
- w_out: bfloat16 [8, 1024, 1024], P('pp', 'tp')
- w_up: bfloat16 [8, 1024, 4096], P('pp', None, 'tp')
- w_down: bfloat16 [8, 4096, 1024], P('pp', 'tp')
Outputs:
- output 1: bfloat16 [16, 512, 1024], P('dp', 'tp', 'pp')
- output 2: bfloat16 [16, 512, 1024], P('dp', 'tp', 'pp')
- output 3: bfloat16 [8, 16, 512, 1024], P('pp', 'dp', 'tp')
All inputs are finite; a program needn't handle non-finite values.
Results may differ from a plain program's by a relative error of at most 0.0179908.
Values are sent between devices in bfloat16 or wider.
A program may use at most 768 MiB of HBM per device.

v0:
```python
import jax
import jax.numpy as jnp
from jax import lax
from jax.sharding import PartitionSpec as P

LN_EPS = 1e-5
ROPE_BASE = 10000.0


def rope_tables(positions, head_dim):
    inv_freq = 1.0 / (ROPE_BASE ** (jnp.arange(0, head_dim, 2).astype(jnp.float32) / head_dim))
    angles = positions.astype(jnp.float32)[:, None] * inv_freq[None, :]
    return jnp.cos(angles), jnp.sin(angles)


def layer_norm(x_in, ln_params):
    x_wide = x_in.astype(jnp.float32)
    centered = x_wide - jnp.mean(x_wide, axis=-1, keepdims=True)
    variance = jnp.mean(jnp.square(centered), axis=-1, keepdims=True)
    return (centered * lax.rsqrt(variance + LN_EPS) * ln_params[0] + ln_params[1]).astype(jnp.bfloat16)


def rotate_half(x_in, cos_tab, sin_tab):
    half_dim = x_in.shape[-1] // 2
    x_wide = x_in.astype(jnp.float32)
    first_half = x_wide[..., :half_dim]
    second_half = x_wide[..., half_dim:]
    return jnp.concatenate([first_half * cos_tab - second_half * sin_tab, second_half * cos_tab + first_half * sin_tab], axis=-1).astype(jnp.bfloat16)


def attention_heads(a_norm, w_qkv, cos_tab, sin_tab):
    groups = w_qkv.shape[1] - 2
    head_dim = w_qkv.shape[2]
    seq_len = a_norm.shape[1]
    qkv_proj = jnp.einsum("nsd,kjhd->nskjh", a_norm, w_qkv, preferred_element_type=jnp.float32).astype(jnp.bfloat16)
    queries = rotate_half(qkv_proj[:, :, :, :groups], cos_tab[:, None, None], sin_tab[:, None, None])
    key_rot = rotate_half(qkv_proj[:, :, :, groups], cos_tab[:, None], sin_tab[:, None])
    values = qkv_proj[:, :, :, groups + 1]
    scores = jnp.einsum("nskgh,ntkh->nkgst", queries, key_rot, preferred_element_type=jnp.float32) * head_dim ** -0.5
    causal = jnp.arange(seq_len)[:, None] >= jnp.arange(seq_len)[None, :]
    attn_probs = jax.nn.softmax(jnp.where(causal, scores, -1e30), axis=-1).astype(jnp.bfloat16)
    return jnp.einsum("nkgst,ntkh->nskgh", attn_probs, values, preferred_element_type=jnp.float32).astype(jnp.bfloat16)


def local_layer(x_loc, ln_attn, ln_mlp, w_qkv, w_out, w_up, w_down, cos_tab, sin_tab):
    x_full = lax.all_gather(x_loc, "tp", axis=1, tiled=True)
    attn_heads = attention_heads(layer_norm(x_full, ln_attn), w_qkv, cos_tab, sin_tab)
    kv_local, groups, head_dim = attn_heads.shape[2], attn_heads.shape[3], attn_heads.shape[4]
    attn_part = jnp.einsum("nskgh,kghd->nsd", attn_heads, w_out.reshape(kv_local, groups, head_dim, w_out.shape[-1]), preferred_element_type=jnp.float32)
    hidden = jax.nn.gelu(jnp.einsum("nsd,df->nsf", layer_norm(x_full, ln_mlp), w_up, preferred_element_type=jnp.float32), approximate=False).astype(jnp.bfloat16)
    mlp_part = jnp.einsum("nsf,fd->nsd", hidden, w_down, preferred_element_type=jnp.float32)
    part_sum = (attn_part + mlp_part).astype(jnp.bfloat16)
    reduced = lax.psum_scatter(part_sum, "tp", scatter_dimension=1, tiled=True)
    return (x_loc.astype(jnp.float32) + reduced.astype(jnp.float32)).astype(jnp.bfloat16)


def solution(mesh):
    stages = mesh.shape["pp"]
    shift_pairs = [(src_stage, src_stage + 1) for src_stage in range(stages - 1)]
    act_spec = P("dp", "tp", None)
    buf_spec = P("pp", "dp", "tp", None)
    emit_spec = P("dp", "tp", "pp")
    stack_spec = P("pp", None, None)

    def stage_body(stage_buf, new_mb, positions, ln_attn, ln_mlp, w_qkv, w_out, w_up, w_down):
        stage_idx = lax.axis_index("pp")
        cos_tab, sin_tab = rope_tables(positions, w_qkv.shape[3])

        def layer_here(x_loc):
            return local_layer(x_loc, ln_attn[0], ln_mlp[0], w_qkv[0], w_out[0], w_up[0], w_down[0], cos_tab, sin_tab)

        def emit_last(y_loc):
            masked = jnp.where(stage_idx == stages - 1, y_loc, jnp.zeros_like(y_loc))
            return lax.psum_scatter(masked, "pp", scatter_dimension=2, tiled=True)

        y_one = layer_here(stage_buf[0])
        emit_one = emit_last(y_one)
        shifted = lax.ppermute(y_one, "pp", shift_pairs)
        buf_one = jnp.where(stage_idx == 0, new_mb, shifted)
        y_two = layer_here(buf_one)
        emit_two = emit_last(y_two)
        final_buf = lax.ppermute(y_two, "pp", shift_pairs)
        return emit_one, emit_two, final_buf[None]

    return jax.shard_map(stage_body, mesh=mesh, in_specs=(buf_spec, act_spec, P(None), stack_spec, stack_spec, P("pp", "tp", None, None, None), P("pp", "tp", None), P("pp", None, "tp"), P("pp", "tp", None)), out_specs=(emit_spec, emit_spec, buf_spec), check_vma=False)
```

profile of v0, /device:TPU:99, one launch (start us, length us, event | category | flops | bytes accessed | tf_op | source)
XLA Modules:
  0.0 1350.9 jit_solution(11073936782367079897)
XLA Ops:
  8.8 0.8 fusion.207
  9.7 1.4 fusion.208
  11.4 153.3 %all-gather.6.cloned.1.call-done = bf16[1,16,512,1024]{3,2,1,0:T(8,128)(2,1)} async-done(((bf16[1,16,128,1024]{3,2,1,0:T(8,128)(2,1)}), bf16[1,16,512,1024]{3,2,1,0:T(8,128)(2,1)}) %all-gather.6.cloned.1.call-update) | async-done | bytes 16777232 | tf_op jit(solution)/shard_map/all_gather | solution.py:46
  164.7 6.8 convert_reduce_fusion
  171.5 7.9 fusion.22
  179.5 20.4 %fusion.89 = bf16[16,512,4,3,64]{1,4,3,2,0:T(8,128)(2,1)} fusion(bf16[1,16,512,1024]{3,2,1,0:T(8,128)(2,1)} %all-gather.6.cloned.1.call-done, f32[1024]{0:T(1024)S(1)} %bitcast.272, f32[1024]{0:T(1024)S(1)} %bitcast.270, f32[16,512]{1,0:T(8,128)S(1)} %add_rsqrt_fusion.1, f32[16,512]{1,0:T(8,128)S(1)} %broadcast_multiply_fusion.1, ...), kind=kOutput, calls=%fused_computation.120 | convolution fusion | flops 12941524992 | bytes 31006720 | tf_op jit(solution)/shard_map/nsd,kjhd->nskjh/dot_general | solution.py:35
  199.9 7.3 slice_convert_fusion.1
  207.2 4.8 fusion.125
  212.0 4.7 fusion.126
  216.7 3.5 subtract_convert_fusion.2
  220.2 26.9 %fusion.2 = (f32[16,4,512]{2,1,0:T(4,128)S(1)}, f32[16,4,512,512]{3,2,1,0:T(8,128)}) fusion(pred[512,512]{0,1:T(8,128)(4,1)S(1)} %iota_compare_fusion, bf16[16,512,4,32]{1,3,2,0:T(8,128)(2,1)} %fusion.126, bf16[16,512,4,32]{1,3,2,0:T(8,128)(2,1)} %fusion.125, bf16[16,512,4,32]{1,3,2,0:T(8,128)(2,1)} %get-tuple-element.21, ...), kind=kOutput, calls=%fused_computation.8 | convolution fusion | flops 2214559744 | bytes 75890688 | tf_op jit(solution)/shard_map/nskgh,ntkh->nkgst/dot_general | solution.py:39
  247.1 21.6 %fusion = f32[16,4,512]{2,1,0:T(4,128)S(1)} fusion(f32[16,4,512,512]{3,2,1,0:T(8,128)} %get-tuple-element.30, f32[16,4,512]{2,1,0:T(4,128)S(1)} %get-tuple-element.29, pred[512,512]{0,1:T(8,128)(4,1)S(1)} %iota_compare_fusion), kind=kLoop, calls=%fused_computation.6 | loop fusion | flops 67076096 | bytes 67633152 | tf_op jit(solution)/shard_map/reduce_sum | solution.py:41
  268.8 30.4 %fusion.229 = bf16[16,512,4,64]{1,3,2,0:T(8,128)(2,1)} fusion(f32[16,4,512]{2,1,0:T(4,128)S(1)} %fusion, f32[16,4,512]{2,1,0:T(4,128)S(1)} %get-tuple-element.29, f32[16,4,512,512]{3,2,1,0:T(8,128)} %get-tuple-element.30, pred[512,512]{0,1:T(8,128)(4,1)S(1)} %iota_compare_fusion, bf16[16,512,4,3,64]{1,4,3,2,0:T(8,128)(2,1)} %fusion.89), kind=kOutput, calls=%fused_computation.146.clone.1 | convolution fusion | flops 2233466880 | bytes 76021760 | tf_op jit(solution)/shard_map/nkgst,ntkh->nskgh/dot_general | solution.py:42
  299.3 37.4 %fusion.75 = (u16[512,1024]{1,0:T(8,128)(2,1)S(1)}, u16[512,1024]{1,0:T(8,128)(2,1)S(1)}, f32[16,512,1024]{2,1,0:T(8,128)}) fusion(bf16[1,1024,1024]{2,1,0:T(8,128)(2,1)S(1)} %copy-done, bf16[1,16,512,1024]{3,2,1,0:T(8,128)(2,1)} %all-gather.6.cloned.1.call-done, f32[1024]{0:T(1024)S(1)} %bitcast.268, f32[1024]{0:T(1024)S(1)} %bitcast.266, ...), kind=kOutput, calls=%fused_computation.108 | convolution fusion | flops 17338204160 | bytes 54599680 | tf_op jit(solution)/shard_map/nsd,df->nsf/dot_general | solution.py:50
  336.7 90.8 %fusion.79 = f32[16,512,1024]{2,1,0:T(8,128)} fusion(f32[16,512,1024]{2,1,0:T(8,128)} %get-tuple-element.28, u16[512,1024]{1,0:T(8,128)(2,1)S(1)} %get-tuple-element.6, u16[512,1024]{1,0:T(8,128)(2,1)S(1)} %get-tuple-element.5, bf16[1,1024,1024]{2,1,0:T(8,128)(2,1)S(1)} %copy-done.23), kind=kOutput, calls=%fused_computation.111 | convolution fusion | flops 17767071744 | bytes 71303168 | tf_op jit(solution)/shard_map/nsf,fd->nsd/dot_general | solution.py:51
  427.5 16.9 %fusion.32 = bf16[16,512,1024]{2,1,0:T(8,128)(2,1)} fusion(f32[16,512,1024]{2,1,0:T(8,128)} %fusion.79, bf16[4,64,1024,1]{2,1,0,3:T(8,128)(2,1)S(1)} %bitcast.274, bf16[16,512,4,64]{1,3,2,0:T(8,128)(2,1)S(1)} %copy-done.28), kind=kOutput, calls=%fused_computation.55 | convolution fusion | flops 4311744512 | bytes 55050240 | tf_op jit(solution)/shard_map/nskgh,kghd->nsd/dot_general | solution.py:49
  444.6 146.5 %reduce-scatter.9.cloned.1.call-done = bf16[16,128,1024]{2,1,0:T(8,128)(2,1)} async-done(((bf16[16,512,1024]{2,1,0:T(8,128)(2,1)}), bf16[16,128,1024]{2,1,0:T(8,128)(2,1)}) %reduce-scatter.9.cloned.1.call-update) | async-done | bytes 4194320 | tf_op jit(solution)/shard_map/reduce_scatter | solution.py:53
  591.1 9.7 broadcast_select_fusion.2
  600.8 3.9 collective-permute-start
  604.7 45.4 %collective-permute-done = bf16[16,128,1024]{2,1,0:T(8,128)(2,1)} collective-permute-done((bf16[16,128,1024]{2,1,0:T(8,128)(2,1)}, bf16[16,128,1024]{2,1,0:T(8,128)(2,1)}, u32[]{:S(2)}, u32[]{:S(2)}) %collective-permute-start) | collective-permute-done | bytes 4194336 | tf_op jit(solution)/shard_map/ppermute | solution.py:78
  650.1 4.6 broadcast_select_fusion
  654.8 152.6 %all-gather.4.cloned.1.call-done = bf16[16,512,1024]{2,1,0:T(8,128)(2,1)} async-done(((bf16[16,128,1024]{2,1,0:T(8,128)(2,1)}), bf16[16,512,1024]{2,1,0:T(8,128)(2,1)}) %all-gather.4.cloned.1.call-update) | async-done | bytes 16777232 | tf_op jit(solution)/shard_map/all_gather | solution.py:46
  807.4 7.2 convert_reduce_fusion.1
  814.7 7.9 fusion.12
  823.2 20.4 %fusion.86 = bf16[16,512,4,3,64]{1,4,2,0,3:T(8,128)(2,1)} fusion(bf16[16,512,1024]{2,1,0:T(8,128)(2,1)} %all-gather.4.cloned.1.call-done, f32[16,512]{1,0:T(8,128)S(1)} %add_rsqrt_fusion, f32[16,512]{1,0:T(8,128)S(1)} %broadcast_multiply_fusion, f32[1024]{0:T(1024)S(1)} %bitcast.273, f32[1024]{0:T(1024)S(1)} %bitcast.271, ...), kind=kOutput, calls=%fused_computation.119 | convolution fusion | flops 12941524992 | bytes 31006720 | tf_op jit(solution)/shard_map/nsd,kjhd->nskjh/dot_general | solution.py:35
  843.7 11.7 slice_convert_fusion
  855.4 6.9 subtract_convert_fusion.1
  862.3 7.0 fusion.123
  869.3 27.1 %fusion.3 = (f32[16,4,512]{2,1,0:T(4,128)S(1)}, f32[16,4,512,512]{3,2,1,0:T(8,128)}) fusion(pred[512,512]{0,1:T(8,128)(4,1)S(1)} %copy-done.2, bf16[16,512,4,32]{1,3,2,0:T(8,128)(2,1)} %get-tuple-element.17, bf16[16,512,4,32]{1,3,2,0:T(8,128)(2,1)} %get-tuple-element.16, bf16[16,512,4,32]{1,3,2,0:T(8,128)(2,1)} %get-tuple-element.19, ...), kind=kOutput, calls=%fused_computation.9 | convolution fusion | flops 2214559744 | bytes 75890688 | tf_op jit(solution)/shard_map/nskgh,ntkh->nkgst/dot_general | solution.py:39
  896.3 21.6 %fusion.1 = f32[16,4,512]{2,1,0:T(4,128)S(1)} fusion(f32[16,4,512,512]{3,2,1,0:T(8,128)} %get-tuple-element.33, f32[16,4,512]{2,1,0:T(4,128)S(1)} %get-tuple-element.32, pred[512,512]{0,1:T(8,128)(4,1)S(1)} %copy-done.2), kind=kLoop, calls=%fused_computation.7 | loop fusion | flops 67076096 | bytes 67633152 | tf_op jit(solution)/shard_map/reduce_sum | solution.py:41
  918.0 30.4 %fusion.226 = bf16[16,512,4,64]{1,3,2,0:T(8,128)(2,1)} fusion(f32[16,4,512]{2,1,0:T(4,128)S(1)} %fusion.1, f32[16,4,512]{2,1,0:T(4,128)S(1)} %get-tuple-element.32, f32[16,4,512,512]{3,2,1,0:T(8,128)} %get-tuple-element.33, pred[512,512]{0,1:T(8,128)(4,1)S(1)} %copy-done.2, bf16[16,512,4,3,64]{1,4,2,0,3:T(8,128)(2,1)} %fusion.86), kind=kOutput, calls=%fused_computation.145.clone.1 | convolution fusion | flops 2233466880 | bytes 76021760 | tf_op jit(solution)/shard_map/nkgst,ntkh->nskgh/dot_general | solution.py:42
  948.4 37.5 %fusion.76 = (u16[512,1024]{1,0:T(8,128)(2,1)S(1)}, u16[512,1024]{1,0:T(8,128)(2,1)S(1)}, f32[16,512,1024]{2,1,0:T(8,128)}) fusion(bf16[1,1024,1024]{2,1,0:T(8,128)(2,1)S(1)} %copy-done, bf16[16,512,1024]{2,1,0:T(8,128)(2,1)} %all-gather.4.cloned.1.call-done, f32[16,512]{1,0:T(8,128)S(1)} %copy-done.12, f32[16,512]{1,0:T(8,128)S(1)} %copy-done.8, ...), kind=kOutput, calls=%fused_computation.109 | convolution fusion | flops 17338204160 | bytes 54599680 | tf_op jit(solution)/shard_map/nsd,df->nsf/dot_general | solution.py:50
  986.0 90.6 %fusion.77 = f32[16,512,1024]{2,1,0:T(8,128)} fusion(f32[16,512,1024]{2,1,0:T(8,128)} %get-tuple-element.31, u16[512,1024]{1,0:T(8,128)(2,1)S(1)} %get-tuple-element.4, u16[512,1024]{1,0:T(8,128)(2,1)S(1)} %get-tuple-element.3, bf16[1,1024,1024]{2,1,0:T(8,128)(2,1)S(1)} %copy-done.24), kind=kOutput, calls=%fused_computation.110 | convolution fusion | flops 17767071744 | bytes 71303168 | tf_op jit(solution)/shard_map/nsf,fd->nsd/dot_general | solution.py:51
  1076.6 17.1 %fusion.29 = bf16[16,512,1024]{2,1,0:T(8,128)(2,1)} fusion(f32[16,512,1024]{2,1,0:T(8,128)} %fusion.77, bf16[4,64,1024,1]{2,1,0,3:T(8,128)(2,1)S(1)} %bitcast.275, bf16[16,512,4,64]{1,3,2,0:T(8,128)(2,1)S(1)} %copy-done.27), kind=kOutput, calls=%fused_computation.51 | convolution fusion | flops 4311744512 | bytes 55050240 | tf_op jit(solution)/shard_map/nskgh,kghd->nsd/dot_general | solution.py:49
  1093.9 6.9 copy.36
  1100.8 6.3 copy.50
  1107.2 133.1 %reduce-scatter.11.cloned.1.call-done = bf16[16,128,1024]{2,1,0:T(8,128)(2,1)} async-done(((bf16[16,512,1024]{2,1,0:T(8,128)(2,1)}), bf16[16,128,1024]{2,1,0:T(8,128)(2,1)}) %reduce-scatter.11.cloned.1.call-update) | async-done | bytes 4194320 | tf_op jit(solution)/shard_map/reduce_scatter | solution.py:53
  1240.4 9.6 broadcast_select_fusion.1
  1250.0 6.9 copy.38
  1256.9 6.3 copy.49
  1263.2 3.9 collective-permute-start.1
  1267.2 10.1 reduce-scatter.13.cloned.1.call-done
  1277.3 1.1 copy.42
  1278.4 1.2 copy.37
  1279.7 56.8 %collective-permute-done.1 = bf16[16,128,1024]{2,1,0:T(8,128)(2,1)} collective-permute-done((bf16[16,128,1024]{2,1,0:T(8,128)(2,1)}, bf16[16,128,1024]{2,1,0:T(8,128)(2,1)}, u32[]{:S(2)}, u32[]{:S(2)}) %collective-permute-start.1) | collective-permute-done | bytes 4194336 | tf_op jit(solution)/shard_map/ppermute | solution.py:82
  1336.5 1.1 copy.44
  1337.6 1.2 copy.39
  1338.8 4.8 copy.52
  (79 shorter events, 3.2 us)
Async XLA Ops:
  7.2 292.1 %copy-start = (bf16[1,1024,1024]{2,1,0:T(8,128)(2,1)S(1)}, bf16[1,1024,1024]{2,1,0:T(8,128)(2,1)}, u32[]{:S(2)}) copy-start(bf16[1,1024,1024]{2,1,0:T(8,128)(2,1)} %param.16) | copy-start | bytes 6291460
  7.2 157.5 %all-gather.6.cloned.1.call-start = ((), (), s32[]{:S(2)}) async-start(), calls=%async_computation.7 | async-start | bytes 20971520 | tf_op jit(solution)/shard_map/all_gather | solution.py:46
  8.0 583.1 %reduce-scatter.9.cloned.1.call-start = ((), (), s32[]{:S(2)}) async-start(), calls=%async_computation.4 | async-start | bytes 20971520 | tf_op jit(solution)/shard_map/reduce_scatter | solution.py:53
  8.8 259.9 %copy-start.1 = (pred[512,512]{0,1:T(8,128)(4,1)}, pred[512,512]{0,1:T(8,128)(4,1)S(1)}, u32[]{:S(2)}) copy-start(pred[512,512]{0,1:T(8,128)(4,1)S(1)} %iota_compare_fusion) | copy-start | bytes 786436
  9.6 190.2 %copy-start.19 = (f32[1,1,1024]{2,1,0:T(1,128)}, f32[1,1,1024]{2,1,0:T(1,128)S(1)}, u32[]{:S(2)}) copy-start(f32[1,1,1024]{2,1,0:T(1,128)S(1)} %get-tuple-element.22) | copy-start | bytes 12292
  9.7 190.2 %copy-start.21 = (f32[1,1,1024]{2,1,0:T(1,128)}, f32[1,1,1024]{2,1,0:T(1,128)S(1)}, u32[]{:S(2)}) copy-start(f32[1,1,1024]{2,1,0:T(1,128)S(1)} %get-tuple-element.23) | copy-start | bytes 12292
  11.4 205.3 %copy-start.3 = (f32[512,32]{0,1:T(8,128)}, f32[512,32]{0,1:T(8,128)S(1)}, u32[]{:S(2)}) copy-start(f32[512,32]{0,1:T(8,128)S(1)} %get-tuple-element.26) | copy-start | bytes 196612
  11.4 205.3 %copy-start.5 = (f32[512,32]{0,1:T(8,128)}, f32[512,32]{0,1:T(8,128)S(1)}, u32[]{:S(2)}) copy-start(f32[512,32]{0,1:T(8,128)S(1)} %get-tuple-element.27) | copy-start | bytes 196612
  171.5 28.4 %copy-start.9 = (f32[16,512]{1,0:T(8,128)}, f32[16,512]{1,0:T(8,128)S(1)}, u32[]{:S(2)}) copy-start(f32[16,512]{1,0:T(8,128)S(1)} %broadcast_multiply_fusion.1) | copy-start | bytes 98308
  179.5 20.4 %copy-start.13 = (f32[16,512]{1,0:T(8,128)}, f32[16,512]{1,0:T(8,128)S(1)}, u32[]{:S(2)}) copy-start(f32[16,512]{1,0:T(8,128)S(1)} %add_rsqrt_fusion.1) | copy-start | bytes 98308
  268.8 30.4 %copy-start.10 = (f32[16,512]{1,0:T(8,128)S(1)}, f32[16,512]{1,0:T(8,128)}, u32[]{:S(2)}) copy-start(f32[16,512]{1,0:T(8,128)} %copy-done.9) | copy-start | bytes 98308
  268.8 30.4 %copy-start.14 = (f32[16,512]{1,0:T(8,128)S(1)}, f32[16,512]{1,0:T(8,128)}, u32[]{:S(2)}) copy-start(f32[16,512]{1,0:T(8,128)} %copy-done.13) | copy-start | bytes 98308
  268.8 30.4 %copy-start.15 = (f32[1,1,1024]{2,1,0:T(1,128)S(1)}, f32[1,1,1024]{2,1,0:T(1,128)}, u32[]{:S(2)}) copy-start(f32[1,1,1024]{2,1,0:T(1,128)} %get-tuple-element.24) | copy-start | bytes 12292
  268.8 30.4 %copy-start.17 = (f32[1,1,1024]{2,1,0:T(1,128)S(1)}, f32[1,1,1024]{2,1,0:T(1,128)}, u32[]{:S(2)}) copy-start(f32[1,1,1024]{2,1,0:T(1,128)} %get-tuple-element.25) | copy-start | bytes 12292
  299.3 37.4 %copy-start.23 = (bf16[1,1024,1024]{2,1,0:T(8,128)(2,1)S(1)}, bf16[1,1024,1024]{2,1,0:T(8,128)(2,1)}, u32[]{:S(2)}) copy-start(bf16[1,1024,1024]{2,1,0:T(8,128)(2,1)} %param.17) | copy-start | bytes 6291460
  336.7 90.9 %copy-start.25 = (bf16[1,256,1024]{2,1,0:T(8,128)(2,1)S(1)}, bf16[1,256,1024]{2,1,0:T(8,128)(2,1)}, u32[]{:S(2)}) copy-start(bf16[1,256,1024]{2,1,0:T(8,128)(2,1)} %param.15) | copy-start | bytes 1572868
  336.7 90.8 %copy-start.28 = (bf16[16,512,4,64]{1,3,2,0:T(8,128)(2,1)S(1)}, bf16[16,512,4,64]{1,3,2,0:T(8,128)(2,1)}, u32[]{:S(2)}) copy-start(bf16[16,512,4,64]{1,3,2,0:T(8,128)(2,1)} %fusion.229) | copy-start | bytes 12582916
  444.5 362.9 %all-gather.4.cloned.1.call-start = ((), (), s32[]{:S(2)}) async-start(), calls=%async_computation.5 | async-start | bytes 20971520 | tf_op jit(solution)/shard_map/all_gather | solution.py:46
  444.6 378.7 %copy-start.20 = (f32[1,1,1024]{2,1,0:T(1,128)S(1)}, f32[1,1,1024]{2,1,0:T(1,128)}, u32[]{:S(2)}) copy-start(f32[1,1,1024]{2,1,0:T(1,128)} %copy-done.19) | copy-start | bytes 12292
  444.6 378.6 %copy-start.22 = (f32[1,1,1024]{2,1,0:T(1,128)S(1)}, f32[1,1,1024]{2,1,0:T(1,128)}, u32[]{:S(2)}) copy-start(f32[1,1,1024]{2,1,0:T(1,128)} %copy-done.21) | copy-start | bytes 12292
  600.8 49.3 %collective-permute-start = (bf16[16,128,1024]{2,1,0:T(8,128)(2,1)}, bf16[16,128,1024]{2,1,0:T(8,128)(2,1)}, u32[]{:S(2)}, u32[]{:S(2)}) collective-permute-start(bf16[16,128,1024]{2,1,0:T(8,128)(2,1)} %get-tuple-element.10), channel_id=1, source_target_pairs={{0,1},{1,2},{2,3},{3,4},{4,5},{5,6},{6,7},{8,9},{9,10},{10,11},{11... | collective-permute-start | bytes 12582920 | tf_op jit(solution)/shard_map/ppermute | solution.py:78
  654.8 585.6 %reduce-scatter.11.cloned.1.call-start = ((), (), s32[]{:S(2)}) async-start(), calls=%async_computation.6 | async-start | bytes 20971520 | tf_op jit(solution)/shard_map/reduce_scatter | solution.py:53
  814.7 8.0 copy-start.7
  822.6 0.6 copy-start.11
  823.2 32.1 %copy-start.4 = (f32[512,32]{0,1:T(8,128)S(1)}, f32[512,32]{0,1:T(8,128)}, u32[]{:S(2)}) copy-start(f32[512,32]{0,1:T(8,128)} %copy-done.3) | copy-start | bytes 196612
  823.2 32.1 %copy-start.6 = (f32[512,32]{0,1:T(8,128)S(1)}, f32[512,32]{0,1:T(8,128)}, u32[]{:S(2)}) copy-start(f32[512,32]{0,1:T(8,128)} %copy-done.5) | copy-start | bytes 196612
  843.7 25.6 %copy-start.2 = (pred[512,512]{0,1:T(8,128)(4,1)S(1)}, pred[512,512]{0,1:T(8,128)(4,1)}, u32[]{:S(2)}) copy-start(pred[512,512]{0,1:T(8,128)(4,1)} %copy-done.1) | copy-start | bytes 786436
  918.0 30.4 %copy-start.8 = (f32[16,512]{1,0:T(8,128)S(1)}, f32[16,512]{1,0:T(8,128)}, u32[]{:S(2)}) copy-start(f32[16,512]{1,0:T(8,128)} %copy-done.7) | copy-start | bytes 98308
  918.0 30.4 %copy-start.12 = (f32[16,512]{1,0:T(8,128)S(1)}, f32[16,512]{1,0:T(8,128)}, u32[]{:S(2)}) copy-start(f32[16,512]{1,0:T(8,128)} %copy-done.11) | copy-start | bytes 98308
  918.0 30.4 %copy-start.16 = (f32[1,1,1024]{2,1,0:T(1,128)S(1)}, f32[1,1,1024]{2,1,0:T(1,128)}, u32[]{:S(2)}) copy-start(f32[1,1,1024]{2,1,0:T(1,128)} %get-tuple-element.24) | copy-start | bytes 12292
  918.0 30.4 %copy-start.18 = (f32[1,1,1024]{2,1,0:T(1,128)S(1)}, f32[1,1,1024]{2,1,0:T(1,128)}, u32[]{:S(2)}) copy-start(f32[1,1,1024]{2,1,0:T(1,128)} %get-tuple-element.25) | copy-start | bytes 12292
  948.4 37.6 %copy-start.24 = (bf16[1,1024,1024]{2,1,0:T(8,128)(2,1)S(1)}, bf16[1,1024,1024]{2,1,0:T(8,128)(2,1)}, u32[]{:S(2)}) copy-start(bf16[1,1024,1024]{2,1,0:T(8,128)(2,1)} %param.17) | copy-start | bytes 6291460
  986.0 90.6 %copy-start.26 = (bf16[1,256,1024]{2,1,0:T(8,128)(2,1)S(1)}, bf16[1,256,1024]{2,1,0:T(8,128)(2,1)}, u32[]{:S(2)}) copy-start(bf16[1,256,1024]{2,1,0:T(8,128)(2,1)} %param.15) | copy-start | bytes 1572868
  986.0 90.6 %copy-start.27 = (bf16[16,512,4,64]{1,3,2,0:T(8,128)(2,1)S(1)}, bf16[16,512,4,64]{1,3,2,0:T(8,128)(2,1)}, u32[]{:S(2)}) copy-start(bf16[16,512,4,64]{1,3,2,0:T(8,128)(2,1)} %fusion.226) | copy-start | bytes 12582916
  1093.8 183.5 %reduce-scatter.13.cloned.1.call-start = ((), (), s32[]{:S(2)}) async-start(), calls=%async_computation.8 | async-start | bytes 4718592
  1107.2 229.3 %reduce-scatter.15.cloned.1.call-start = ((), (), s32[]{:S(2)}) async-start(), calls=%async_computation.9 | async-start | bytes 4718592
  1263.2 73.2 %collective-permute-start.1 = (bf16[16,128,1024]{2,1,0:T(8,128)(2,1)}, bf16[16,128,1024]{2,1,0:T(8,128)(2,1)}, u32[]{:S(2)}, u32[]{:S(2)}) collective-permute-start(bf16[16,128,1024]{2,1,0:T(8,128)(2,1)} %get-tuple-element.8), channel_id=1, source_target_pairs={{0,1},{1,2},{2,3},{3,4},{4,5},{5,6},{6,7},{8,9},{9,10},{10,11},{11... | collective-permute-start | bytes 12582920 | tf_op jit(solution)/shard_map/ppermute | solution.py:82
Sparse Core Ops, SparseCore 0:
  9.6 155.0 all-gather.5
  444.6 146.3 reduce-scatter.8
  654.9 152.5 all-gather.3
  1093.9 146.3 reduce-scatter.10
  1243.1 34.1 reduce-scatter.12
  1279.4 50.1 reduce-scatter.14
where the time goes:
time: 1360 us; the launch traced here: 1350 us
  waiting for transfers between devices  699 us (51%)
  matrix products  446 us (33%)
  other arithmetic  144 us (11%)
  local copies, waits for them, and re-layouts  38.9 us (3%)
  between operations  15 us (1%)
    all_gather x2, waiting for transfers between devices, local_layer(): x_full = lax.all_gather(x_loc, 'tp', axis=1, tiled=True)  306 us
    reduce_scatter x2, waiting for transfers between devices, local_layer(): reduced = lax.psum_scatter(part_sum, 'tp', scatter_dimension=1, tiled=True)  280 us
    dot_general x2, matrix products, local_layer(): jnp.einsum('nsf,fd->nsd', hidden, w_down, preferred_element_type=jnp.floa...  181 us
    dot_general x2, matrix products, local_layer(): jnp.einsum('nsd,df->nsf', layer_norm(x_full, ln_mlp), w_up, preferred_ele...  74.9 us
    dot_general x2, matrix products, attention_heads(): jnp.einsum('nkgst,ntkh->nskgh', attn_probs, values, preferred_element_typ...  60.8 us
    ppermute x1, waiting for transfers between devices, stage_body(): final_buf = lax.ppermute(y_two, 'pp', shift_pairs)  56.8 us
    dot_general x2, matrix products, attention_heads(): jnp.einsum('nskgh,ntkh->nkgst', queries, key_rot, preferred_element_type=...  53.9 us
    ppermute x1, waiting for transfers between devices, stage_body(): shifted = lax.ppermute(y_one, 'pp', shift_pairs)  45.4 us
  transfers between devices with their start and end apart: 8, of which 7 were waited for; matrix products, arithmetic and copies ran while one was open for 3% of the time, Pallas kernels for 0%

commit v1 on v0

v1 whole, which is shorter than its diff:
```python
import functools
import math

import jax
import jax.numpy as jnp
from jax import lax
from jax.experimental import pallas as pl
from jax.experimental.pallas import tpu as pltpu
from jax.sharding import PartitionSpec as P

LN_EPS = 1e-5
ROPE_BASE = 10000.0
F32 = jnp.float32
BF16 = jnp.bfloat16
MESH = pl.DeviceIdType.MESH
LN_ROWS = 64
Q_BLK = 128
COL = 256


def nt_dot(lhs, rhs):
    return lax.dot_general(lhs, rhs, (((1,), (1,)), ((), ())), preferred_element_type=F32)


def nn_dot(lhs, rhs):
    return jnp.dot(lhs, rhs, preferred_element_type=F32)


def gelu(pre):
    return 0.5 * pre * (1.0 + lax.erf(pre * math.sqrt(0.5)))


def normalise(dims, x_ref, acc_ref, a_ref, m_ref, ln_ref):
    def body(i, carry):
        rows = pl.ds(pl.multiple_of(i * LN_ROWS, LN_ROWS), LN_ROWS)
        wide = x_ref[rows, :].astype(F32)
        acc_ref[rows, :] = wide
        centered = wide - jnp.mean(wide, axis=-1, keepdims=True)
        var = jnp.mean(jnp.square(centered), axis=-1, keepdims=True)
        normed = centered * lax.rsqrt(var + LN_EPS)
        a_ref[rows, :] = (normed * ln_ref[0:1, :] + ln_ref[1:2, :]).astype(BF16)
        m_ref[rows, :] = (normed * ln_ref[2:3, :] + ln_ref[3:4, :]).astype(BF16)
        return carry

    lax.fori_loop(0, dims[0] // LN_ROWS, body, 0)


def add_quarter(dims, a_ref, m_ref, w, acc_ref, cos_ref, sin_ref, q_s, k_s, v_s, km_s, vm_s, o_s, h_s):
    seq, width, heads, head_dim, ff = dims
    qk_w = heads * head_dim
    half_w = qk_w // 2
    qkv_rows = 3 * qk_w
    qkv = nt_dot(a_ref[...], w[0:qkv_rows, :])
    qk = qkv[:, :2 * qk_w].astype(BF16).astype(F32)
    cos = cos_ref[...]
    sin = sin_ref[...]
    for dst, lo in ((q_s, 0), (k_s, qk_w)):
        first_half = qk[:, lo:lo + half_w]
        second_half = qk[:, lo + half_w:lo + qk_w]
        dst[:, :half_w] = (first_half * cos - second_half * sin).astype(BF16)
        dst[:, half_w:] = (second_half * cos + first_half * sin).astype(BF16)
    v_s[...] = qkv[:, 2 * qk_w:].astype(BF16)
    o_s[...] = jnp.zeros_like(o_s)

    exp_scale = math.log2(math.e) * head_dim ** -0.5
    lane = lax.broadcasted_iota(jnp.int32, (1, qk_w), 1)
    key_head = (lane % half_w) // (head_dim // 2)
    value_head = lane // head_dim
    causal = lax.broadcasted_iota(jnp.int32, (Q_BLK, Q_BLK), 0) >= lax.broadcasted_iota(jnp.int32, (Q_BLK, Q_BLK), 1)

    def head_body(h, carry):
        km_s[...] = k_s[...] * jnp.where(key_head == h, 1.0, 0.0).astype(BF16)
        vm_s[...] = v_s[...] * jnp.where(value_head == h, 1.0, 0.0).astype(BF16)
        for blk in range(seq // Q_BLK):
            lo = blk * Q_BLK
            hi = lo + Q_BLK
            s_diag = jnp.where(causal, nt_dot(q_s[lo:hi, :], km_s[lo:hi, :]), -1e30)
            top = jnp.max(s_diag, axis=-1, keepdims=True)
            if blk:
                s_past = nt_dot(q_s[lo:hi, :], km_s[0:lo, :])
                top = jnp.maximum(top, jnp.max(s_past, axis=-1, keepdims=True))
            e_diag = jnp.exp2((s_diag - top) * exp_scale)
            tot = jnp.sum(e_diag, axis=-1, keepdims=True)
            if blk:
                e_past = jnp.exp2((s_past - top) * exp_scale)
                tot = tot + jnp.sum(e_past, axis=-1, keepdims=True)
            inv = 1.0 / tot
            o_blk = nn_dot((e_diag * inv).astype(BF16), vm_s[lo:hi, :])
            if blk:
                o_blk = o_blk + nn_dot((e_past * inv).astype(BF16), vm_s[0:lo, :])
            o_s[lo:hi, :] += o_blk
        return carry

    lax.fori_loop(0, heads, head_body, 0)
    h_s[:, 0:qk_w] = o_s[...].astype(BF16)

    for j in range(ff // COL):
        pre = nn_dot(m_ref[...], w[qkv_rows:qkv_rows + width, j * COL:(j + 1) * COL])
        h_s[:, qk_w + j * COL:qk_w + (j + 1) * COL] = gelu(pre).astype(BF16)
    out0 = qkv_rows + width
    for j in range(width // COL):
        acc_ref[:, j * COL:(j + 1) * COL] += nn_dot(h_s[...], w[out0:out0 + qk_w + ff, j * COL:(j + 1) * COL])


def ticks_kernel(dims, ranks, stages, stage_ref, mb_ref, own_ref, ln_ref, cos_ref, sin_ref, emit_one, emit_two, final_ref,
                 wbuf, xs, acc, a_s, m_s, q_s, k_s, v_s, km_s, vm_s, o_s, h_s, zero_s,
                 x_send, x_recv, mb_send, w_send, w_recv, y_send, out_send, out_recv):
    seq, width = dims[:2]
    seq_loc = seq // ranks
    blk = xs.shape[1]
    cols = width // stages
    half = wbuf.shape[1] // 2
    y = lax.axis_index("tp")
    p = lax.axis_index("pp")
    chip = p // 2
    core = p % 2
    role = (y // 2 + chip) % 2
    layer = 2 * chip + role
    last = layer == stages - 1
    home = core == role
    sibling = p + 1 - 2 * core
    mate = y + 1 - 2 * (y % 2)
    across = ranks - 1 - y
    block_one = 2 * (y % 2) + core
    block_two = jnp.where(role == 0, block_one, 2 * (1 - y % 2) + core)
    my_seq = pl.ds(pl.multiple_of(y * seq_loc, seq_loc), seq_loc)
    my_half = pl.ds(pl.multiple_of(core * half, half), half)

    def remote(src, dst, send, recv, tp, pp):
        return pltpu.make_async_remote_copy(src_ref=src, dst_ref=dst, send_sem=send, recv_sem=recv, device_id={"tp": tp, "pp": pp}, device_id_type=MESH)

    def put(src, dst, send, recv, tp, pp):
        here = jnp.logical_and(tp == y, pp == p)

        @pl.when(here)
        def _():
            pltpu.make_async_copy(src, dst, recv).start()

        @pl.when(jnp.logical_not(here))
        def _():
            remote(src, dst, send, recv, tp, pp).start()

    def wait_bytes(like, sem):
        pltpu.make_async_copy(like, like, sem).wait()

    own_copy = pltpu.make_async_copy(own_ref, wbuf.at[0], w_recv.at[0])
    own_send = remote(own_ref, wbuf.at[0], w_send.at[0], w_recv.at[0], y, sibling)

    @pl.when(home)
    def _():
        own_copy.start()
        own_send.start()

    pair_of_stage = (core + chip) % 2

    def send_x(i, carry):
        for b in range(ranks):
            put(stage_ref.at[b * blk + i], xs.at[0, i, my_seq], x_send, x_recv.at[0, i], 2 * pair_of_stage + b // 2, 2 * chip + b % 2)
        return carry

    lax.fori_loop(0, blk, send_x, 0)

    @pl.when(home)
    def _():
        for h in range(2):
            part = pl.ds(h * half, half)
            remote(own_ref.at[part], wbuf.at[1, part], w_send.at[1], w_recv.at[1], mate, 2 * chip + h).start()

    @pl.when(jnp.logical_not(home))
    def _():
        for h in range(2):
            part = pl.ds(h * half, half)
            remote(own_ref.at[part], wbuf.at[2, part], w_send.at[1], w_recv.at[3], across, 2 * chip + h).start()

    @pl.when(p == 0)
    def _():
        zero_s[...] = jnp.zeros_like(zero_s)

        def put_zero(n, carry):
            pltpu.make_async_copy(zero_s, final_ref.at[n], out_recv.at[0]).start()
            return carry

        lax.fori_loop(0, blk * ranks, put_zero, 0)

    mate_swap = [remote(wbuf.at[slot, my_half], wbuf.at[slot, my_half], w_send.at[1 + slot], w_recv.at[2 * slot], y, sibling) for slot in range(1, 4)]
    pass_on = remote(wbuf.at[2, my_half], wbuf.at[3, my_half], w_send.at[5], w_recv.at[5], mate, p)

    def before_slot(slot):
        if slot == 0:
            wait_bytes(wbuf.at[0], w_recv.at[0])
        elif slot == 1:
            wait_bytes(wbuf.at[2, my_half], w_recv.at[3])
            pass_on.start()
            mate_swap[1].start()
            wait_bytes(wbuf.at[1, my_half], w_recv.at[1])
            mate_swap[0].start()

            @pl.when(chip == 0)
            def _():
                def send_mb(i, carry):
                    for b in range(ranks // 2):
                        put(mb_ref.at[(2 * b + core) * blk + i], xs.at[1, i, my_seq], mb_send, x_recv.at[1, i], b, core)
                    return carry

                lax.fori_loop(0, blk, send_mb, 0)

            wait_bytes(wbuf.at[1, my_half], w_recv.at[2])
        elif slot == 2:
            wait_bytes(wbuf.at[2, my_half], w_recv.at[4])
        else:
            wait_bytes(wbuf.at[3, my_half], w_recv.at[5])
            mate_swap[2].start()
            wait_bytes(wbuf.at[3, my_half], w_recv.at[6])

    def send_emit(tick, dst, rows, row0, block):
        def body(n, carry):
            tp, pp = n // stages, n % stages
            src = xs.at[tick, pl.ds(row0, rows), pl.ds(pl.multiple_of(tp * seq_loc, seq_loc), seq_loc), pl.ds(pl.multiple_of(pp * cols, cols), cols)]
            put(src, dst.at[pl.ds(block * blk + row0, rows)], out_send, out_recv.at[1 + tick], tp, pp)
            return carry

        lax.fori_loop(0, ranks * stages, body, 0)

    steps = blk * ranks

    def step_body(step, carry):
        tick = step // steps
        index = step % steps
        slot = jnp.where(tick == 0, index // blk, index % ranks)
        row = jnp.where(tick == 0, index % blk, index // ranks)
        for s in range(ranks):
            @pl.when(step == s * blk)
            def _(s=s):
                before_slot(s)

        @pl.when(slot == 0)
        def _():
            wait_bytes(xs.at[tick, row], x_recv.at[tick, row])
            normalise(dims, xs.at[tick, row], acc.at[row], a_s.at[row], m_s.at[row], ln_ref)

        add_quarter(dims, a_s.at[row], m_s.at[row], wbuf.at[slot], acc.at[row], cos_ref, sin_ref, q_s, k_s, v_s, km_s, vm_s, o_s, h_s)

        @pl.when(slot == ranks - 1)
        def _():
            xs[tick, row] = acc[row].astype(BF16)

            @pl.when(jnp.logical_and(tick == 0, jnp.logical_not(last)))
            def _():
                next_y = jnp.where(role == 0, across, y)
                next_p = jnp.where(role == 0, p, p + 2)
                remote(xs.at[0, row], xs.at[1, row], y_send, x_recv.at[1, row], next_y, next_p).start()

            @pl.when(jnp.logical_and(step == steps - 1, last))
            def _():
                send_emit(0, emit_one, blk, 0, block_one)

            @pl.when(jnp.logical_and(tick == 1, last))
            def _():
                send_emit(1, emit_two, 1, row, block_two)

            @pl.when(jnp.logical_and(tick == 1, jnp.logical_not(last)))
            def _():
                def send_final(n, carry):
                    part = pl.ds(pl.multiple_of(n * seq_loc, seq_loc), seq_loc)
                    put(xs.at[1, row, part], final_ref.at[block_two * blk + row], out_send, out_recv.at[0], n, layer + 1)
                    return carry

                lax.fori_loop(0, ranks, send_final, 0)

        return carry

    lax.fori_loop(0, 2 * steps, step_body, 0)

    wait_bytes(stage_ref.at[pl.ds(0, (ranks - 1) * blk)], x_send)

    @pl.when(home)
    def _():
        wait_bytes(own_ref, w_send.at[0])

    @pl.when(jnp.logical_not(home))
    def _():
        wait_bytes(stage_ref.at[pl.ds(0, blk)], x_send)

    wait_bytes(own_ref, w_send.at[1])
    for slot in range(2, 6):
        wait_bytes(wbuf.at[1, my_half], w_send.at[slot])

    @pl.when(chip == 0)
    def _():
        wait_bytes(mb_ref.at[pl.ds(0, blk)], mb_send)

        @pl.when(role == 1)
        def _():
            wait_bytes(mb_ref.at[pl.ds(0, blk)], mb_send)

    @pl.when(jnp.logical_not(last))
    def _():
        wait_bytes(xs.at[0], y_send)
        wait_bytes(xs.at[1, :, pl.ds(0, seq - seq_loc)], out_send)

        @pl.when(p != layer + 1)
        def _():
            wait_bytes(xs.at[1, :, pl.ds(0, seq_loc)], out_send)

    @pl.when(last)
    def _():
        wait_bytes(xs.at[:, :, pl.ds(0, seq - seq_loc)], out_send)
        wait_bytes(xs.at[:, :, pl.ds(0, seq_loc), pl.ds(0, width - cols)], out_send)

    wait_bytes(final_ref, out_recv.at[0])
    wait_bytes(emit_one, out_recv.at[1])
    wait_bytes(emit_two, out_recv.at[2])


def rope_tables(positions, head_dim, heads):
    inv_freq = 1.0 / (ROPE_BASE ** (jnp.arange(0, head_dim, 2).astype(F32) / head_dim))
    angles = positions.astype(F32)[:, None] * inv_freq[None, :]
    return jnp.tile(jnp.cos(angles), (1, heads)), jnp.tile(jnp.sin(angles), (1, heads))


def pack_weights(w_qkv, w_out, w_up, w_down):
    heads, _, head_dim, width = w_qkv.shape
    halves = w_qkv.reshape(heads, 3, 2, head_dim // 2, width)
    qk = halves[:, :2].transpose(1, 2, 0, 3, 4).reshape(-1, width)
    values = w_qkv[:, 2].reshape(-1, width)
    return jnp.concatenate([qk, values, w_up, w_out, w_down], axis=0)


def solution(mesh):
    stages = mesh.shape["pp"]
    ranks = mesh.shape["tp"]

    def stage_body(stage_buf, new_mb, positions, ln_attn, ln_mlp, w_qkv, w_out, w_up, w_down):
        mb, seq_loc, width = new_mb.shape
        seq = seq_loc * ranks
        blk = mb // ranks
        heads, head_dim = w_qkv.shape[1], w_qkv.shape[3]
        ff = w_up.shape[2]
        dims = (seq, width, heads, head_dim, ff)
        qk_w = heads * head_dim
        cos_tab, sin_tab = rope_tables(positions, head_dim, heads)
        lns = jnp.concatenate([ln_attn[0], ln_mlp[0]], axis=0)
        stage = lax.axis_index("pp")
        role = (lax.axis_index("tp") // 2 + stage // 2) % 2
        other = lax.ppermute(lns, "pp", [(s, s + 1 - 2 * (s % 2)) for s in range(stages)])
        lns = jnp.where(stage % 2 == role, lns, other)
        own = pack_weights(w_qkv[0], w_out[0], w_up[0], w_down[0])
        hbm = pl.BlockSpec(memory_space=pltpu.HBM)
        vmem = pl.BlockSpec(memory_space=pltpu.VMEM)
        dma = pltpu.SemaphoreType.DMA
        emit = jax.ShapeDtypeStruct((mb, seq_loc, width // stages), BF16)
        emit_one, emit_two, final_buf = pl.pallas_call(
            functools.partial(ticks_kernel, dims, ranks, stages),
            out_shape=(emit, emit, jax.ShapeDtypeStruct((mb, seq_loc, width), BF16)),
            in_specs=[hbm, hbm, hbm, vmem, vmem, vmem],
            out_specs=(hbm, hbm, hbm),
            scratch_shapes=[
                pltpu.VMEM((ranks,) + own.shape, BF16),
                pltpu.VMEM((2, blk, seq, width), BF16),
                pltpu.VMEM((blk, seq, width), F32),
                pltpu.VMEM((blk, seq, width), BF16),
                pltpu.VMEM((blk, seq, width), BF16),
                pltpu.VMEM((seq, qk_w), BF16),
                pltpu.VMEM((seq, qk_w), BF16),
                pltpu.VMEM((seq, qk_w), BF16),
                pltpu.VMEM((seq, qk_w), BF16),
                pltpu.VMEM((seq, qk_w), BF16),
                pltpu.VMEM((seq, qk_w), F32),
                pltpu.VMEM((seq, qk_w + ff), BF16),
                pltpu.VMEM((seq_loc, width), BF16),
                dma, dma((2, blk)), dma, dma((6,)), dma((7,)), dma, dma, dma((3,)),
            ],
            compiler_params=pltpu.CompilerParams(has_side_effects=True, vmem_limit_bytes=63 * 1000 * 1024),
        )(stage_buf[0], new_mb, own, lns, cos_tab, sin_tab)
        return emit_one, emit_two, final_buf[None]

    act_spec = P("dp", "tp", None)
    buf_spec = P("pp", "dp", "tp", None)
    emit_spec = P("dp", "tp", "pp")
    stack_spec = P("pp", None, None)
    return jax.shard_map(stage_body, mesh=mesh, in_specs=(buf_spec, act_spec, P(None), stack_spec, stack_spec, P("pp", "tp", None, None, None), P("pp", "tp", None), P("pp", None, "tp"), P("pp", "tp", None)), out_specs=(emit_spec, emit_spec, buf_spec), check_vma=False)
```

time: 1360 us -> 476 us (0.35)
  waiting for transfers between devices: 699 us -> 0.01 us
  Pallas kernels: 0 us -> 454 us
  matrix products: 446 us -> 0 us
  other arithmetic: 144 us -> 1.81 us
  local copies, waits for them, and re-layouts: 38.9 us -> 18.5 us
  between operations: 15 us -> 0.79 us
    pallas_call x0 -> x1, Pallas kernels: none -> 454 us  [stage_body(): pl.pallas_call(functools.partial(ticks_kernel, dims, ranks, stages), out_...]
    dot_general x12 -> x0, matrix products: 446 us -> none  [the longest x2 181 us: local_layer(): jnp.einsum('nsf,fd->nsd', hidden, w_down, preferred_element_type=jnp.floa...]
    all_gather x2 -> x0, waiting for transfers between devices: 306 us -> none  [local_layer(): x_full = lax.all_gather(x_loc, 'tp', axis=1, tiled=True)]
    reduce_scatter x2 -> x0, waiting for transfers between devices: 280 us -> none  [local_layer(): reduced = lax.psum_scatter(part_sum, 'tp', scatter_dimension=1, tiled=True)]
    ppermute x2 -> x1, waiting for transfers between devices: 102 us -> 0.01 us  [stage_body(): lax.ppermute(lns, 'pp', [(s, s + 1 - 2 * (s % 2)) for s in range(stages)])]
    reduce_sum x6 -> x0, other arithmetic: 73.2 us -> none  [the longest x2 43.3 us: attention_heads(): jax.nn.softmax(jnp.where(causal, scores, -1e+30), axis=-1)]
    unnamed x67 -> x20, local copies, waits for them, and re-layouts: 36.7 us -> 12.9 us
    select_n x3 -> x1, other arithmetic: 23.9 us -> 0.62 us  [stage_body(): lns = jnp.where(stage % 2 == role, lns, other)]
  transfers between devices with their start and end apart: 8 -> 1, of which waited for: 7 -> 0; matrix products, arithmetic and copies ran while one was open for 3% -> 2% of each run, Pallas kernels for 0% -> 0%
where the time goes in v1:
time: 476 us
  Pallas kernels  454 us (95%)
  local copies, waits for them, and re-layouts  18.5 us (4%)
    pallas_call x1, Pallas kernels, stage_body(): pl.pallas_call(functools.partial(ticks_kernel, dims, ranks, stages), out_...  454 us
    unnamed x20, local copies, waits for them, and re-layouts  12.9 us
  transfers between devices with their start and end apart: 1, of which 0 were waited for; matrix products, arithmetic and copies ran while one was open for 2% of the time, Pallas kernels for 0%

profile of v1, /device:TPU:99, one launch (start us, length us, event | category | flops | bytes accessed | tf_op | source)
XLA Modules:
  0.0 476.1 jit_solution(15121354075063575028)
XLA Ops:
  0.6 0.0 copy-start.5
  0.6 0.0 copy-start
  0.7 0.9 pad_maximum_fusion
  1.5 0.7 collective-permute-start
  2.2 0.0 copy-start.2
  2.2 1.4 slice.8
  3.6 0.0 copy-start.1
  3.6 0.1 copy.16
  3.7 1.0 constant_dynamic-update-slice_fusion.1
  4.8 1.1 slice.9
  5.9 0.0 copy-done.5
  5.9 0.0 copy-start.3
  5.9 0.0 copy-start.4
  5.9 0.8 constant_dynamic-update-slice_fusion
  6.7 0.0 copy-done
  6.7 1.5 bitcast_dynamic-update-slice_fusion.1
  8.2 0.0 copy-done.2
  8.2 0.8 bitcast_dynamic-update-slice_fusion.2
  9.0 0.0 copy-done.1
  9.0 1.5 bitcast_dynamic-update-slice_fusion.own_ref
  10.5 0.3 multiply_sine_fusion
  10.9 0.8 copy.14.cos_ref
  11.8 0.8 copy.15.sin_ref
  12.6 0.0 collective-permute-done
  12.6 0.0 copy-done.3
  12.6 0.0 copy-done.4
  12.6 0.6 broadcast_select_fusion.ln_ref
  13.2 454.2 %shard_map.112 = (bf16[16,128,128]{2,1,0:T(8,128)(2,1)}, bf16[16,128,128]{2,1,0:T(8,128)(2,1)}, bf16[16,128,1024]{2,1,0:T(8,128)(2,1)}) custom-call(bf16[16,128,1024]{2,1,0:T(8,128)(2,1)} %bitcast.18, bf16[16,128,1024]{2,1,0:T(8,128)(2,1)} %mb_ref.1, bf16[3072,1024]{1,0:T(8,128)(2,1)} %bitcast_dynamic-update-slice_fusion.own_ref, ...), custom_call_target="tpu_custom_call" | custom-call | tf_op jit(solution)/shard_map/pallas_call | solution.py:352
  467.5 1.9 copy.24
  469.4 1.9 copy.25
  471.3 4.8 %copy.26 = bf16[1,16,128,1024]{3,2,1,0:T(8,128)(2,1)} copy(bf16[1,16,128,1024]{3,2,1,0:T(8,128)(2,1)} %bitcast.19) | data formatting | bytes 8388608
  (4 shorter events, 0.0 us)
Async XLA Ops:
  0.6 5.2 %copy-start.5 = (s32[512]{0:T(512)S(1)}, s32[512]{0:T(512)}, u32[]{:S(2)}) copy-start(s32[512]{0:T(512)} %param.11) | copy-start | bytes 6148
  0.6 6.1 %copy-start = (bf16[1,1024,1024]{2,1,0:T(8,128)(2,1)S(1)}, bf16[1,1024,1024]{2,1,0:T(8,128)(2,1)}, u32[]{:S(2)}) copy-start(bf16[1,1024,1024]{2,1,0:T(8,128)(2,1)} %param.16) | copy-start | bytes 6291460
  1.5 11.1 %collective-permute-start = (f32[4,1024]{1,0:T(4,128)S(1)}, f32[4,1024]{1,0:T(4,128)S(1)}, u32[]{:S(2)}, u32[]{:S(2)}) collective-permute-start(f32[4,1024]{1,0:T(4,128)S(1)} %pad_maximum_fusion), channel_id=1, source_target_pairs={{0,1},{1,0},{2,3},{3,2},{4,5},{5,4},{6,7},{7,6},{8,9},{9,8},{10,11... | collective-permute-start | bytes 49160 | tf_op jit(solution)/shard_map/ppermute | solution.py:345
  2.2 6.0 %copy-start.2 = (bf16[1,256,1024]{2,1,0:T(8,128)(2,1)S(1)}, bf16[1,256,1024]{2,1,0:T(8,128)(2,1)}, u32[]{:S(2)}) copy-start(bf16[1,256,1024]{2,1,0:T(8,128)(2,1)} %param.15) | copy-start | bytes 1572868
  3.6 5.4 %copy-start.1 = (bf16[1,1024,1024]{2,1,0:T(8,128)(2,1)S(1)}, bf16[1,1024,1024]{2,1,0:T(8,128)(2,1)}, u32[]{:S(2)}) copy-start(bf16[1,1024,1024]{2,1,0:T(8,128)(2,1)} %param.17) | copy-start | bytes 6291460
  5.9 6.8 %copy-start.3 = (f32[1,2,1024]{2,1,0:T(2,128)S(1)}, f32[1,2,1024]{2,1,0:T(2,128)}, u32[]{:S(2)}) copy-start(f32[1,2,1024]{2,1,0:T(2,128)} %param.13) | copy-start | bytes 24580
  5.9 6.8 %copy-start.4 = (f32[1,2,1024]{2,1,0:T(2,128)S(1)}, f32[1,2,1024]{2,1,0:T(2,128)}, u32[]{:S(2)}) copy-start(f32[1,2,1024]{2,1,0:T(2,128)} %param.12) | copy-start | bytes 24580

commit v2 on v1

--- a/solution.py
+++ b/solution.py
@@ -14,7 +14,8 @@
 BF16 = jnp.bfloat16
 MESH = pl.DeviceIdType.MESH
 LN_ROWS = 64
-Q_BLK = 128
+Q_BLK = 256
+HEAD_UNROLL = 2
 COL = 256
 
 
@@ -24,6 +25,10 @@
 
 def nn_dot(lhs, rhs):
     return jnp.dot(lhs, rhs, preferred_element_type=F32)
+
+
+def tn_dot(lhs, rhs):
+    return lax.dot_general(lhs, rhs, (((0,), (0,)), ((), ())), preferred_element_type=F32)
 
 
 def gelu(pre):
@@ -38,61 +43,58 @@
         centered = wide - jnp.mean(wide, axis=-1, keepdims=True)
         var = jnp.mean(jnp.square(centered), axis=-1, keepdims=True)
         normed = centered * lax.rsqrt(var + LN_EPS)
-        a_ref[rows, :] = (normed * ln_ref[0:1, :] + ln_ref[1:2, :]).astype(BF16)
-        m_ref[rows, :] = (normed * ln_ref[2:3, :] + ln_ref[3:4, :]).astype(BF16)
+        a_ref[rows, :] = (normed * ln_ref[0, 0:1, :] + ln_ref[0, 1:2, :]).astype(BF16)
+        m_ref[rows, :] = (normed * ln_ref[1, 0:1, :] + ln_ref[1, 1:2, :]).astype(BF16)
         return carry
 
     lax.fori_loop(0, dims[0] // LN_ROWS, body, 0)
 
 
-def add_quarter(dims, a_ref, m_ref, w, acc_ref, cos_ref, sin_ref, q_s, k_s, v_s, km_s, vm_s, o_s, h_s):
+def add_quarter(dims, a_ref, m_ref, w, acc_ref, cos_ref, sin_ref, q_s, k_s, v_s, o_s, h_s):
     seq, width, heads, head_dim, ff = dims
     qk_w = heads * head_dim
-    half_w = qk_w // 2
     qkv_rows = 3 * qk_w
-    qkv = nt_dot(a_ref[...], w[0:qkv_rows, :])
-    qk = qkv[:, :2 * qk_w].astype(BF16).astype(F32)
+    hd2 = head_dim // 2
+    qkv = nt_dot(w[0:qkv_rows, :], a_ref[...]).astype(BF16)
     cos = cos_ref[...]
     sin = sin_ref[...]
-    for dst, lo in ((q_s, 0), (k_s, qk_w)):
-        first_half = qk[:, lo:lo + half_w]
-        second_half = qk[:, lo + half_w:lo + qk_w]
-        dst[:, :half_w] = (first_half * cos - second_half * sin).astype(BF16)
-        dst[:, half_w:] = (second_half * cos + first_half * sin).astype(BF16)
-    v_s[...] = qkv[:, 2 * qk_w:].astype(BF16)
-    o_s[...] = jnp.zeros_like(o_s)
+    for h in range(heads):
+        base = 3 * h * head_dim
+        for dst, lo in ((q_s, base), (k_s, base + head_dim)):
+            first_half = qkv[lo:lo + hd2].astype(F32)
+            second_half = qkv[lo + hd2:lo + head_dim].astype(F32)
+            dst[h * head_dim:h * head_dim + hd2, :] = (first_half * cos - second_half * sin).astype(BF16)
+            dst[h * head_dim + hd2:(h + 1) * head_dim, :] = (second_half * cos + first_half * sin).astype(BF16)
+        v_s[h * head_dim:(h + 1) * head_dim, :] = qkv[base + 2 * head_dim:base + 3 * head_dim]
 
     exp_scale = math.log2(math.e) * head_dim ** -0.5
-    lane = lax.broadcasted_iota(jnp.int32, (1, qk_w), 1)
-    key_head = (lane % half_w) // (head_dim // 2)
-    value_head = lane // head_dim
-    causal = lax.broadcasted_iota(jnp.int32, (Q_BLK, Q_BLK), 0) >= lax.broadcasted_iota(jnp.int32, (Q_BLK, Q_BLK), 1)
+    causal = lax.broadcasted_iota(jnp.int32, (Q_BLK, Q_BLK), 0) <= lax.broadcasted_iota(jnp.int32, (Q_BLK, Q_BLK), 1)
 
     def head_body(h, carry):
-        km_s[...] = k_s[...] * jnp.where(key_head == h, 1.0, 0.0).astype(BF16)
-        vm_s[...] = v_s[...] * jnp.where(value_head == h, 1.0, 0.0).astype(BF16)
+        rows = pl.ds(pl.multiple_of(h * head_dim, head_dim), head_dim)
         for blk in range(seq // Q_BLK):
             lo = blk * Q_BLK
             hi = lo + Q_BLK
-            s_diag = jnp.where(causal, nt_dot(q_s[lo:hi, :], km_s[lo:hi, :]), -1e30)
-            top = jnp.max(s_diag, axis=-1, keepdims=True)
+            query = q_s[rows, lo:hi]
+            s_diag = jnp.where(causal, tn_dot(k_s[rows, lo:hi], query), -1e30)
+            top = jnp.max(s_diag, axis=0, keepdims=True)
             if blk:
-                s_past = nt_dot(q_s[lo:hi, :], km_s[0:lo, :])
-                top = jnp.maximum(top, jnp.max(s_past, axis=-1, keepdims=True))
+                s_past = tn_dot(k_s[rows, 0:lo], query)
+                top = jnp.maximum(top, jnp.max(s_past, axis=0, keepdims=True))
             e_diag = jnp.exp2((s_diag - top) * exp_scale)
-            tot = jnp.sum(e_diag, axis=-1, keepdims=True)
+            tot = jnp.sum(e_diag, axis=0, keepdims=True)
             if blk:
                 e_past = jnp.exp2((s_past - top) * exp_scale)
-                tot = tot + jnp.sum(e_past, axis=-1, keepdims=True)
+                tot = tot + jnp.sum(e_past, axis=0, keepdims=True)
             inv = 1.0 / tot
-            o_blk = nn_dot((e_diag * inv).astype(BF16), vm_s[lo:hi, :])
+            o_blk = nn_dot(v_s[rows, lo:hi], (e_diag * inv).astype(BF16))
             if blk:
-                o_blk = o_blk + nn_dot((e_past * inv).astype(BF16), vm_s[0:lo, :])
-            o_s[lo:hi, :] += o_blk
+                o_blk = o_blk + nn_dot(v_s[rows, 0:lo], (e_past * inv).astype(BF16))
+            o_s[rows, lo:hi] = o_blk
         return carry
 
-    lax.fori_loop(0, heads, head_body, 0)
-    h_s[:, 0:qk_w] = o_s[...].astype(BF16)
+    lax.fori_loop(0, heads, head_body, 0, unroll=HEAD_UNROLL)
+    h_s[:, 0:qk_w] = jnp.transpose(o_s[...]).astype(BF16)
 
     for j in range(ff // COL):
         pre = nn_dot(m_ref[...], w[qkv_rows:qkv_rows + width, j * COL:(j + 1) * COL])
@@ -102,9 +104,9 @@
         acc_ref[:, j * COL:(j + 1) * COL] += nn_dot(h_s[...], w[out0:out0 + qk_w + ff, j * COL:(j + 1) * COL])
 
 
-def ticks_kernel(dims, ranks, stages, stage_ref, mb_ref, own_ref, ln_ref, cos_ref, sin_ref, emit_one, emit_two, final_ref,
-                 wbuf, xs, acc, a_s, m_s, q_s, k_s, v_s, km_s, vm_s, o_s, h_s, zero_s,
-                 x_send, x_recv, mb_send, w_send, w_recv, y_send, out_send, out_recv):
+def ticks_kernel(dims, ranks, stages, stage_ref, mb_ref, qkv_ref, up_ref, wo_ref, down_ref, ln_attn_ref, ln_mlp_ref, cos_ref, sin_ref,
+                 emit_one, emit_two, final_ref, wbuf, xs, acc, a_s, m_s, q_s, k_s, v_s, o_s, h_s, zero_s, ln_s,
+                 x_send, x_recv, mb_send, w_send, w_recv, y_send, out_send, out_recv, ln_send, ln_recv):
     seq, width = dims[:2]
     seq_loc = seq // ranks
     blk = xs.shape[1]
@@ -143,13 +145,22 @@
     def wait_bytes(like, sem):
         pltpu.make_async_copy(like, like, sem).wait()
 
-    own_copy = pltpu.make_async_copy(own_ref, wbuf.at[0], w_recv.at[0])
-    own_send = remote(own_ref, wbuf.at[0], w_send.at[0], w_recv.at[0], y, sibling)
+    def own_parts(lo, hi):
+        start = 0
+        for ref in (qkv_ref, up_ref, wo_ref, down_ref):
+            first, end = max(lo, start), min(hi, start + ref.shape[0])
+            if first < end:
+                yield ref.at[pl.ds(first - start, end - first)], pl.ds(first, end - first)
+            start += ref.shape[0]
 
     @pl.when(home)
     def _():
-        own_copy.start()
-        own_send.start()
+        for i, ref in enumerate((ln_attn_ref, ln_mlp_ref)):
+            pltpu.make_async_copy(ref, ln_s.at[i], ln_recv).start()
+            remote(ref, ln_s.at[i], ln_send, ln_recv, y, sibling).start()
+        for src, part in own_parts(0, 2 * half):
+            pltpu.make_async_copy(src, wbuf.at[0, part], w_recv.at[0]).start()
+            remote(src, wbuf.at[0, part], w_send.at[0], w_recv.at[0], y, sibling).start()
 
     pair_of_stage = (core + chip) % 2
 
@@ -163,14 +174,14 @@
     @pl.when(home)
     def _():
         for h in range(2):
-            part = pl.ds(h * half, half)
-            remote(own_ref.at[part], wbuf.at[1, part], w_send.at[1], w_recv.at[1], mate, 2 * chip + h).start()
+            for src, part in own_parts(h * half, (h + 1) * half):
+                remote(src, wbuf.at[1, part], w_send.at[1], w_recv.at[1], mate, 2 * chip + h).start()
 
     @pl.when(jnp.logical_not(home))
     def _():
         for h in range(2):
-            part = pl.ds(h * half, half)
-            remote(own_ref.at[part], wbuf.at[2, part], w_send.at[1], w_recv.at[3], across, 2 * chip + h).start()
+            for src, part in own_parts(h * half, (h + 1) * half):
+                remote(src, wbuf.at[2, part], w_send.at[1], w_recv.at[3], across, 2 * chip + h).start()
 
     @pl.when(p == 0)
     def _():
@@ -187,6 +198,7 @@
 
     def before_slot(slot):
         if slot == 0:
+            wait_bytes(ln_s, ln_recv)
             wait_bytes(wbuf.at[0], w_recv.at[0])
         elif slot == 1:
             wait_bytes(wbuf.at[2, my_half], w_recv.at[3])
@@ -236,9 +248,9 @@
         @pl.when(slot == 0)
         def _():
             wait_bytes(xs.at[tick, row], x_recv.at[tick, row])
-            normalise(dims, xs.at[tick, row], acc.at[row], a_s.at[row], m_s.at[row], ln_ref)
-
-        add_quarter(dims, a_s.at[row], m_s.at[row], wbuf.at[slot], acc.at[row], cos_ref, sin_ref, q_s, k_s, v_s, km_s, vm_s, o_s, h_s)
+            normalise(dims, xs.at[tick, row], acc.at[row], a_s.at[row], m_s.at[row], ln_s)
+
+        add_quarter(dims, a_s.at[row], m_s.at[row], wbuf.at[slot], acc.at[row], cos_ref, sin_ref, q_s, k_s, v_s, o_s, h_s)
 
         @pl.when(slot == ranks - 1)
         def _():
@@ -275,13 +287,14 @@
 
     @pl.when(home)
     def _():
-        wait_bytes(own_ref, w_send.at[0])
+        wait_bytes(ln_s, ln_send)
+        wait_bytes(wbuf.at[0], w_send.at[0])
 
     @pl.when(jnp.logical_not(home))
     def _():
         wait_bytes(stage_ref.at[pl.ds(0, blk)], x_send)
 
-    wait_bytes(own_ref, w_send.at[1])
+    wait_bytes(wbuf.at[0], w_send.at[1])
     for slot in range(2, 6):
         wait_bytes(wbuf.at[1, my_half], w_send.at[slot])
 
@@ -312,18 +325,10 @@
     wait_bytes(emit_two, out_recv.at[2])
 
 
-def rope_tables(positions, head_dim, heads):
+def rope_tables(positions, head_dim):
     inv_freq = 1.0 / (ROPE_BASE ** (jnp.arange(0, head_dim, 2).astype(F32) / head_dim))
-    angles = positions.astype(F32)[:, None] * inv_freq[None, :]
-    return jnp.tile(jnp.cos(angles), (1, heads)), jnp.tile(jnp.sin(angles), (1, heads))
-
-
-def pack_weights(w_qkv, w_out, w_up, w_down):
-    heads, _, head_dim, width = w_qkv.shape
-    halves = w_qkv.reshape(heads, 3, 2, head_dim // 2, width)
-    qk = halves[:, :2].transpose(1, 2, 0, 3, 4).reshape(-1, width)
-    values = w_qkv[:, 2].reshape(-1, width)
-    return jnp.concatenate([qk, values, w_up, w_out, w_down], axis=0)
+    angles = inv_freq[:, None] * positions.astype(F32)[None, :]
+    return jnp.cos(angles), jnp.sin(angles)
 
 
 def solution(mesh):
@@ -338,13 +343,8 @@
         ff = w_up.shape[2]
         dims = (seq, width, heads, head_dim, ff)
         qk_w = heads * head_dim
-        cos_tab, sin_tab = rope_tables(positions, head_dim, heads)
-        lns = jnp.concatenate([ln_attn[0], ln_mlp[0]], axis=0)
-        stage = lax.axis_index("pp")
-        role = (lax.axis_index("tp") // 2 + stage // 2) % 2
-        other = lax.ppermute(lns, "pp", [(s, s + 1 - 2 * (s % 2)) for s in range(stages)])
-        lns = jnp.where(stage % 2 == role, lns, other)
-        own = pack_weights(w_qkv[0], w_out[0], w_up[0], w_down[0])
+        cos_tab, sin_tab = rope_tables(positions, head_dim)
+        slot_rows = 4 * qk_w + width + ff
         hbm = pl.BlockSpec(memory_space=pltpu.HBM)
         vmem = pl.BlockSpec(memory_space=pltpu.VMEM)
         dma = pltpu.SemaphoreType.DMA
@@ -352,26 +352,25 @@
         emit_one, emit_two, final_buf = pl.pallas_call(
             functools.partial(ticks_kernel, dims, ranks, stages),
             out_shape=(emit, emit, jax.ShapeDtypeStruct((mb, seq_loc, width), BF16)),
-            in_specs=[hbm, hbm, hbm, vmem, vmem, vmem],
+            in_specs=[hbm] * 8 + [vmem] * 2,
             out_specs=(hbm, hbm, hbm),
             scratch_shapes=[
-                pltpu.VMEM((ranks,) + own.shape, BF16),
+                pltpu.VMEM((ranks, slot_rows, width), BF16),
                 pltpu.VMEM((2, blk, seq, width), BF16),
                 pltpu.VMEM((blk, seq, width), F32),
                 pltpu.VMEM((blk, seq, width), BF16),
                 pltpu.VMEM((blk, seq, width), BF16),
-                pltpu.VMEM((seq, qk_w), BF16),
-                pltpu.VMEM((seq, qk_w), BF16),
-                pltpu.VMEM((seq, qk_w), BF16),
-                pltpu.VMEM((seq, qk_w), BF16),
-                pltpu.VMEM((seq, qk_w), BF16),
-                pltpu.VMEM((seq, qk_w), F32),
+                pltpu.VMEM((qk_w, seq), BF16),
+                pltpu.VMEM((qk_w, seq), BF16),
+                pltpu.VMEM((qk_w, seq), BF16),
+                pltpu.VMEM((qk_w, seq), F32),
                 pltpu.VMEM((seq, qk_w + ff), BF16),
                 pltpu.VMEM((seq_loc, width), BF16),
-                dma, dma((2, blk)), dma, dma((6,)), dma((7,)), dma, dma, dma((3,)),
+                pltpu.VMEM((2, 2, width), F32),
+                dma, dma((2, blk)), dma, dma((6,)), dma((7,)), dma, dma, dma((3,)), dma, dma,
             ],
             compiler_params=pltpu.CompilerParams(has_side_effects=True, vmem_limit_bytes=63 * 1000 * 1024),
-        )(stage_buf[0], new_mb, own, lns, cos_tab, sin_tab)
+        )(stage_buf[0], new_mb, w_qkv[0].reshape(3 * qk_w, width), w_up[0], w_out[0], w_down[0], ln_attn[0], ln_mlp[0], cos_tab, sin_tab)
         return emit_one, emit_two, final_buf[None]
 
     act_spec = P("dp", "tp", None)

time: 476 us -> 412 us (0.87)
  Pallas kernels: 454 us -> 401 us
  local copies, waits for them, and re-layouts: 18.5 us -> 8.57 us
    pallas_call x1, Pallas kernels: 454 us -> 401 us  [stage_body(): pl.pallas_call(functools.partial(ticks_kernel, dims, ranks, stages), out_...]
    unnamed x20 -> x3, local copies, waits for them, and re-layouts: 12.9 us -> 8.57 us
  transfers between devices with their start and end apart: 1 -> 0, of which waited for: 0 -> 0; matrix products, arithmetic and copies ran while one was open for 2% -> 0% of each run, Pallas kernels for 0% -> 0%
where the time goes in v2:
time: 412 us
  Pallas kernels  401 us (97%)
  local copies, waits for them, and re-layouts  8.57 us (2%)
    pallas_call x1, Pallas kernels, stage_body(): pl.pallas_call(functools.partial(ticks_kernel, dims, ranks, stages), out_...  401 us
    unnamed x3, local copies, waits for them, and re-layouts  8.57 us

profile of v2, /device:TPU:99, one launch (start us, length us, event | category | flops | bytes accessed | tf_op | source)
XLA Modules:
  0.0 411.5 jit_solution(4550684460595129035)
XLA Ops:
  0.6 0.7 convert_element_type.11
  1.3 1.0 multiply_sine_fusion
  2.3 400.7 %shard_map.112 = (bf16[16,128,128]{2,1,0:T(8,128)(2,1)}, bf16[16,128,128]{2,1,0:T(8,128)(2,1)}, bf16[16,128,1024]{2,1,0:T(8,128)(2,1)}) custom-call(bf16[16,128,1024]{2,1,0:T(8,128)(2,1)} %bitcast.8, bf16[16,128,1024]{2,1,0:T(8,128)(2,1)} %mb_ref.1, bf16[768,1024]{1,0:T(8,128)(2,1)} %bitcast.12, bf16[1024,1024]{1,0:T(8,128)(2,1)} %bitcast.10, ...), custom_call_target="tpu_custom_call" | custom-call | tf_op jit(solution)/shard_map/pallas_call | solution.py:352
  403.0 1.9 copy.15
  404.9 1.9 copy.16
  406.7 4.8 %copy.17 = bf16[1,16,128,1024]{3,2,1,0:T(8,128)(2,1)} copy(bf16[1,16,128,1024]{3,2,1,0:T(8,128)(2,1)} %bitcast.9) | data formatting | bytes 8388608
  (1 shorter events, 0.0 us)

commit v3 on v2

--- a/solution.py
+++ b/solution.py
@@ -15,7 +15,7 @@
 MESH = pl.DeviceIdType.MESH
 LN_ROWS = 64
 Q_BLK = 256
-HEAD_UNROLL = 2
+HEAD_UNROLL = 4
 COL = 256
 
 
@@ -105,8 +105,8 @@
 
 
 def ticks_kernel(dims, ranks, stages, stage_ref, mb_ref, qkv_ref, up_ref, wo_ref, down_ref, ln_attn_ref, ln_mlp_ref, cos_ref, sin_ref,
-                 emit_one, emit_two, final_ref, wbuf, xs, acc, a_s, m_s, q_s, k_s, v_s, o_s, h_s, zero_s, ln_s,
-                 x_send, x_recv, mb_send, w_send, w_recv, y_send, out_send, out_recv, ln_send, ln_recv):
+                 emit_one, emit_two, final_ref, wbuf, xs, acc, a_s, m_s, q_s, k_s, v_s, o_s, h_s, zero_s, ln_s, relay_s,
+                 x_send, x_recv, mb_send, w_send, w_recv, y_send, out_send, out_recv, ln_send, ln_recv, relay_send, relay_recv):
     seq, width = dims[:2]
     seq_loc = seq // ranks
     blk = xs.shape[1]
@@ -162,26 +162,54 @@
             pltpu.make_async_copy(src, wbuf.at[0, part], w_recv.at[0]).start()
             remote(src, wbuf.at[0, part], w_send.at[0], w_recv.at[0], y, sibling).start()
 
-    pair_of_stage = (core + chip) % 2
-
-    def send_x(i, carry):
-        for b in range(ranks):
-            put(stage_ref.at[b * blk + i], xs.at[0, i, my_seq], x_send, x_recv.at[0, i], 2 * pair_of_stage + b // 2, 2 * chip + b % 2)
-        return carry
-
-    lax.fori_loop(0, blk, send_x, 0)
+    def x_part(block, i):
+        return stage_ref.at[block * blk + i]
+
+    def send_home(i):
+        for b in range(2):
+            remote(x_part(2 * (mate % 2) + b, i), xs.at[0, i, my_seq], x_send, x_recv.at[0, i], mate, 2 * chip + b).start()
+
+    def relay(i):
+        wait_bytes(relay_s.at[pl.ds(2 * i, 2)], relay_recv.at[i])
+        seq_across = pl.ds(pl.multiple_of(across * seq_loc, seq_loc), seq_loc)
+        for b in range(2):
+            remote(relay_s.at[2 * i + b], xs.at[0, i, seq_across], relay_send, x_recv.at[0, i], mate, 2 * chip + b).start()
 
     @pl.when(home)
     def _():
-        for h in range(2):
-            for src, part in own_parts(h * half, (h + 1) * half):
-                remote(src, wbuf.at[1, part], w_send.at[1], w_recv.at[1], mate, 2 * chip + h).start()
+        def keep(i, carry):
+            pltpu.make_async_copy(x_part(2 * (y % 2) + core, i), xs.at[0, i, my_seq], x_recv.at[0, i]).start()
+            remote(x_part(2 * (y % 2) + 1 - core, i), xs.at[0, i, my_seq], x_send, x_recv.at[0, i], y, sibling).start()
+            return carry
+
+        lax.fori_loop(0, blk, keep, 0)
+        for i in range(2):
+            send_home(i)
 
     @pl.when(jnp.logical_not(home))
     def _():
+        def send_across(i, carry):
+            for b in range(2):
+                remote(x_part(2 * (1 - across % 2) + b, i), relay_s.at[2 * i + b], x_send, relay_recv.at[i], across, p).start()
+            for b in range(2):
+                remote(x_part(2 * (across % 2) + b, i), xs.at[0, i, my_seq], x_send, x_recv.at[0, i], across, 2 * chip + b).start()
+            return carry
+
+        lax.fori_loop(0, blk, send_across, 0)
         for h in range(2):
             for src, part in own_parts(h * half, (h + 1) * half):
                 remote(src, wbuf.at[2, part], w_send.at[1], w_recv.at[3], across, 2 * chip + h).start()
+
+    def relay_step(i):
+        @pl.when(home)
+        def _():
+            relay(i)
+            if i + 2 < blk:
+                send_home(i + 2)
+            if i == blk - 1:
+                for h in range(2):
+                    for src, part in own_parts(h * half, (h + 1) * half):
+                        remote(src, wbuf.at[1, part], w_send.at[1], w_recv.at[1], mate, 2 * chip + h).start()
 
     @pl.when(p == 0)
     def _():
@@ -207,6 +235,13 @@
             wait_bytes(wbuf.at[1, my_half], w_recv.at[1])
             mate_swap[0].start()
 
+            wait_bytes(wbuf.at[1, my_half], w_recv.at[2])
+        elif slot == 2:
+            wait_bytes(wbuf.at[2, my_half], w_recv.at[4])
+        else:
+            wait_bytes(wbuf.at[3, my_half], w_recv.at[5])
+            mate_swap[2].start()
+
             @pl.when(chip == 0)
             def _():
                 def send_mb(i, carry):
@@ -216,12 +251,6 @@
 
                 lax.fori_loop(0, blk, send_mb, 0)
 
-            wait_bytes(wbuf.at[1, my_half], w_recv.at[2])
-        elif slot == 2:
-            wait_bytes(wbuf.at[2, my_half], w_recv.at[4])
-        else:
-            wait_bytes(wbuf.at[3, my_half], w_recv.at[5])
-            mate_swap[2].start()
             wait_bytes(wbuf.at[3, my_half], w_recv.at[6])
 
     def send_emit(tick, dst, rows, row0, block):
@@ -245,6 +274,11 @@
             def _(s=s):
                 before_slot(s)
 
+        for i in range(blk):
+            @pl.when(step == i)
+            def _(i=i):
+                relay_step(i)
+
         @pl.when(slot == 0)
         def _():
             wait_bytes(xs.at[tick, row], x_recv.at[tick, row])
@@ -288,6 +322,7 @@
     @pl.when(home)
     def _():
         wait_bytes(ln_s, ln_send)
+        wait_bytes(relay_s, relay_send)
         wait_bytes(wbuf.at[0], w_send.at[0])
 
     @pl.when(jnp.logical_not(home))
@@ -367,7 +402,8 @@
                 pltpu.VMEM((seq, qk_w + ff), BF16),
                 pltpu.VMEM((seq_loc, width), BF16),
                 pltpu.VMEM((2, 2, width), F32),
-                dma, dma((2, blk)), dma, dma((6,)), dma((7,)), dma, dma, dma((3,)), dma, dma,
+                pltpu.VMEM((2 * blk, seq_loc, width), BF16),
+                dma, dma((2, blk)), dma, dma((6,)), dma((7,)), dma, dma, dma((3,)), dma, dma, dma, dma((blk,)),
             ],
             compiler_params=pltpu.CompilerParams(has_side_effects=True, vmem_limit_bytes=63 * 1000 * 1024),
         )(stage_buf[0], new_mb, w_qkv[0].reshape(3 * qk_w, width), w_up[0], w_out[0], w_down[0], ln_attn[0], ln_mlp[0], cos_tab, sin_tab)

time: 412 us -> 430 us (1.044)
  Pallas kernels: 401 us -> 419 us
    pallas_call x1, Pallas kernels: 401 us -> 419 us  [stage_body(): pl.pallas_call(functools.partial(ticks_kernel, dims, ranks, stages), out_...]
where the time goes in v3:
time: 430 us
  Pallas kernels  419 us (97%)
  local copies, waits for them, and re-layouts  8.57 us (2%)
    pallas_call x1, Pallas kernels, stage_body(): pl.pallas_call(functools.partial(ticks_kernel, dims, ranks, stages), out_...  419 us

profile of v3, /device:TPU:99, one launch (start us, length us, event | category | flops | bytes accessed | tf_op | source)
XLA Modules:
  0.0 429.5 jit_solution(14188832744879601945)
XLA Ops:
  0.6 0.7 convert_element_type.11
  1.3 1.0 multiply_sine_fusion
  2.3 418.6 %shard_map.112 = (bf16[16,128,128]{2,1,0:T(8,128)(2,1)}, bf16[16,128,128]{2,1,0:T(8,128)(2,1)}, bf16[16,128,1024]{2,1,0:T(8,128)(2,1)}) custom-call(bf16[16,128,1024]{2,1,0:T(8,128)(2,1)} %bitcast.8, bf16[16,128,1024]{2,1,0:T(8,128)(2,1)} %mb_ref.1, bf16[768,1024]{1,0:T(8,128)(2,1)} %bitcast.12, bf16[1024,1024]{1,0:T(8,128)(2,1)} %bitcast.10, ...), custom_call_target="tpu_custom_call" | custom-call | tf_op jit(solution)/shard_map/pallas_call | solution.py:387
  421.0 1.9 copy.15
  422.8 1.9 copy.16
  424.7 4.8 %copy.17 = bf16[1,16,128,1024]{3,2,1,0:T(8,128)(2,1)} copy(bf16[1,16,128,1024]{3,2,1,0:T(8,128)(2,1)} %bitcast.9) | data formatting | bytes 8388608
  (1 shorter events, 0.0 us)

commit v4 on v2

--- a/solution.py
+++ b/solution.py
@@ -15,7 +15,7 @@
 MESH = pl.DeviceIdType.MESH
 LN_ROWS = 64
 Q_BLK = 256
-HEAD_UNROLL = 2
+HEAD_UNROLL = 4
 COL = 256
 
 
@@ -201,21 +201,8 @@
             wait_bytes(ln_s, ln_recv)
             wait_bytes(wbuf.at[0], w_recv.at[0])
         elif slot == 1:
-            wait_bytes(wbuf.at[2, my_half], w_recv.at[3])
-            pass_on.start()
-            mate_swap[1].start()
             wait_bytes(wbuf.at[1, my_half], w_recv.at[1])
             mate_swap[0].start()
-
-            @pl.when(chip == 0)
-            def _():
-                def send_mb(i, carry):
-                    for b in range(ranks // 2):
-                        put(mb_ref.at[(2 * b + core) * blk + i], xs.at[1, i, my_seq], mb_send, x_recv.at[1, i], b, core)
-                    return carry
-
-                lax.fori_loop(0, blk, send_mb, 0)
-
             wait_bytes(wbuf.at[1, my_half], w_recv.at[2])
         elif slot == 2:
             wait_bytes(wbuf.at[2, my_half], w_recv.at[4])
@@ -245,6 +232,21 @@
             def _(s=s):
                 before_slot(s)
 
+        @pl.when(step == blk + blk // 2)
+        def _():
+            wait_bytes(wbuf.at[2, my_half], w_recv.at[3])
+            pass_on.start()
+            mate_swap[1].start()
+
+            @pl.when(chip == 0)
+            def _():
+                def send_mb(i, carry):
+                    for b in range(ranks // 2):
+                        put(mb_ref.at[(2 * b + core) * blk + i], xs.at[1, i, my_seq], mb_send, x_recv.at[1, i], b, core)
+                    return carry
+
+                lax.fori_loop(0, blk, send_mb, 0)
+
         @pl.when(slot == 0)
         def _():
             wait_bytes(xs.at[tick, row], x_recv.at[tick, row])
@@ -262,7 +264,7 @@
                 next_p = jnp.where(role == 0, p, p + 2)
                 remote(xs.at[0, row], xs.at[1, row], y_send, x_recv.at[1, row], next_y, next_p).start()
 
-            @pl.when(jnp.logical_and(step == steps - 1, last))
+            @pl.when(jnp.logical_and(step == steps + 2 * ranks - 1, last))
             def _():
                 send_emit(0, emit_one, blk, 0, block_one)
 

time: 412 us -> 428 us (1.039)
  the two profiles are of different devices: /device:TPU:99 before, /device:TPU:126 now
where the time goes in v4:
time: 428 us; the launch traced here: 427 us
  Pallas kernels  417 us (97%)
  local copies, waits for them, and re-layouts  8.57 us (2%)
    pallas_call x1, Pallas kernels, stage_body(): pl.pallas_call(functools.partial(ticks_kernel, dims, ranks, stages), out_...  417 us
    unnamed x3, local copies, waits for them, and re-layouts  8.57 us

profile of v4, /device:TPU:126, one launch (start us, length us, event | category | flops | bytes accessed | tf_op | source)
XLA Modules:
  0.0 427.5 jit_solution(4257969262724440973)
XLA Ops:
  0.6 0.7 convert_element_type.11
  1.3 1.0 multiply_sine_fusion
  2.3 416.6 %shard_map.112 = (bf16[16,128,128]{2,1,0:T(8,128)(2,1)}, bf16[16,128,128]{2,1,0:T(8,128)(2,1)}, bf16[16,128,1024]{2,1,0:T(8,128)(2,1)}) custom-call(bf16[16,128,1024]{2,1,0:T(8,128)(2,1)} %bitcast.8, bf16[16,128,1024]{2,1,0:T(8,128)(2,1)} %mb_ref.1, bf16[768,1024]{1,0:T(8,128)(2,1)} %bitcast.12, bf16[1024,1024]{1,0:T(8,128)(2,1)} %bitcast.10, ...), custom_call_target="tpu_custom_call" | custom-call | tf_op jit(solution)/shard_map/pallas_call | solution.py:354
  418.9 1.9 copy.15
  420.8 1.9 copy.16
  422.7 4.8 %copy.17 = bf16[1,16,128,1024]{3,2,1,0:T(8,128)(2,1)} copy(bf16[1,16,128,1024]{3,2,1,0:T(8,128)(2,1)} %bitcast.9) | data formatting | bytes 8388608
  (1 shorter events, 0.0 us)
